TPU v7x, 32 devices: a whole 2x2x4 slice. The times are simulated.
32 devices in a mesh: pop: 8 (over z, x), mp: 4 (over y, core).
Axes of the slice: x: 2, y: 2, z: 4, core: 2. Of those that a mesh axis runs over, the one named last changes fastest.
Arguments:
- tokens: bfloat16 [256, 3584], replicated, may hold values from -60 to 60
- target: bfloat16 [256, 3584], P(None, 'mp'), may hold values from -6 to 6
- w_query: bfloat16 [3584, 3584], P('pop', 'mp'), may hold values from -0.09375 to 0.09375
- w_key: bfloat16 [3584, 512], P(None, 'mp'), may hold values from -0.09375 to 0.09375
- w_value: bfloat16 [3584, 512], P(None, 'mp'), may hold values from -0.09375 to 0.09375
- w_out: bfloat16 [3584, 3584], P('mp', 'pop'), may hold values from -0.09375 to 0.09375
- query_left_factors: bfloat16 [8, 3584, 4], P('pop'), may hold values from -0.09375 to 0.09375
- query_right_factors: bfloat16 [8, 4, 3584], P('pop', None, 'mp'), may hold values from -6 to 6
- o_left: bfloat16 [8, 3584, 4], P('pop', 'mp'), may hold values from -0.09375 to 0.09375
- o_right: bfloat16 [8, 4, 3584], P('pop'), may hold values from -6 to 6
- member_ids: int32 [8], P('pop'), may hold values from 0 to 7, each once
Outputs:
- grad_query: float32 [3584, 3584], P('pop', 'mp')
- grad_out: float32 [3584, 3584], P('mp', 'pop')
- fitness: float32 [8], P('pop')
Inputs may be any that keep to these rules, and one draw needn't show every extreme that they name: `member_ids`: every number from 0 to 7 appears once.
All inputs are finite; a program needn't handle non-finite values.
Results may differ from a plain program's by a relative error of at most 0.005.
Values may be sent and summed in bfloat16 or wider, within the bound.
A program may use at most 64 MiB of HBM per device.

v0:
```python
import math
import jax
import jax.numpy as jnp
from jax import lax
from jax.sharding import PartitionSpec as P

D = 3584
HEADS = 28
KV_HEADS = 4
HEAD_DIM = 128
RANK = 4
noise_scale = 0.5
rope_base = 1000000.0
spread_floor = 0.001


def tables(count, head_size):
    position = jnp.arange(count, dtype=jnp.float32)
    index = jnp.arange(head_size // 2, dtype=jnp.float32)
    freq = jnp.exp(-math.log(rope_base) * 2.0 * index / head_size)
    angle = position[:, None] * freq[None, :]
    return (jnp.cos(angle)[:, None, :], jnp.sin(angle)[:, None, :])


def rotate(field, cosine_table, sine):
    half = field.shape[-1] // 2
    first = field[..., :half]
    second = field[..., half:]
    return jnp.concatenate(
        [first * cosine_table - second * sine, second * cosine_table + first * sine], axis=-1
    )


def per_device(
    tokens,
    target,
    w_query,
    w_key,
    w_value,
    w_out,
    query_left_factors,
    query_right_factors,
    o_left,
    o_right,
    member_ids,
):
    tok = tokens.shape[0]
    local_feats = w_query.shape[1]
    local_kv = w_key.shape[1] // HEAD_DIM
    group = HEADS // KV_HEADS
    local_heads = local_kv * group
    slots = query_left_factors.shape[0]
    scale = HEAD_DIM ** (-0.5)
    cosine_table, sine = tables(tok, HEAD_DIM)
    base = jnp.dot(
        tokens,
        lax.all_gather(w_query, "pop", axis=0, tiled=True),
        preferred_element_type=jnp.float32,
    )
    keys = rotate(
        jnp.dot(tokens, w_key, preferred_element_type=jnp.float32).reshape(tok, local_kv, HEAD_DIM),
        cosine_table,
        sine,
    ).astype(jnp.bfloat16)
    values = (
        jnp.dot(tokens, w_value, preferred_element_type=jnp.float32)
        .astype(jnp.bfloat16)
        .reshape(tok, local_kv, HEAD_DIM)
    )
    signs = (1 - 2 * (member_ids % 2)).astype(jnp.float32)
    factor = noise_scale * signs[:, None, None]
    lowrank_product = jnp.einsum(
        "td,mdr->mtr", tokens, query_left_factors, preferred_element_type=jnp.float32
    ).astype(jnp.bfloat16)
    query = base[None] + factor * jnp.einsum(
        "olj,ojv->olv", lowrank_product, query_right_factors, preferred_element_type=jnp.float32
    )
    query = rotate(
        query.reshape(slots, tok, local_heads, HEAD_DIM), cosine_table[None], sine[None]
    ).astype(jnp.bfloat16)
    query = query.reshape(slots, tok, local_kv, group, HEAD_DIM)
    scores = jnp.einsum("mtkgd,skd->mkgts", query, keys, preferred_element_type=jnp.float32) * scale
    causal = jnp.arange(tok)[:, None] >= jnp.arange(tok)[None, :]
    scores = jnp.where(causal, scores, -1e30)
    probs = jax.nn.softmax(scores, axis=-1).astype(jnp.bfloat16)
    mixed = (
        jnp.einsum("mkgts,skd->mtkgd", probs, values, preferred_element_type=jnp.float32)
        .astype(jnp.bfloat16)
        .reshape(slots, tok, local_feats)
    )
    low_out = jnp.einsum("mtf,mfr->mtr", mixed, o_left, preferred_element_type=jnp.float32)
    right_full = o_right.astype(jnp.float32)
    part = jnp.einsum(
        "mtf,fe->mte",
        mixed,
        lax.all_gather(w_out, "pop", axis=1, tiled=True),
        preferred_element_type=jnp.float32,
    )
    term = part + factor * jnp.einsum(
        "mtr,mre->mte", low_out, right_full, precision=lax.Precision.HIGHEST
    )
    output = lax.psum_scatter(
        term.astype(jnp.bfloat16), "mp", scatter_dimension=2, tiled=True
    ).astype(jnp.float32)
    diff = output - target.astype(jnp.float32)[None]
    errors = lax.psum(jnp.sum(diff * diff, axis=(1, 2)), "mp")
    fitness = -(errors / (tok * D))
    count = slots * lax.axis_size("pop")
    mean = lax.psum(jnp.sum(fitness), "pop") / count
    spread = lax.psum(jnp.sum((fitness - mean) * (fitness - mean)), "pop") / count
    weight = signs * (fitness - mean) / jnp.sqrt(spread + spread_floor)
    every_weight = lax.all_gather(weight, "pop", axis=0, tiled=True)
    right_factors_gathered, left_all = (
        lax.all_gather(query_right_factors, "pop", axis=0, tiled=True),
        lax.all_gather(o_left, "pop", axis=0, tiled=True),
    )
    rows_q = lax.all_to_all(query_left_factors, "pop", split_axis=1, concat_axis=0, tiled=True)
    cols_o = lax.all_to_all(o_right, "pop", split_axis=2, concat_axis=0, tiled=True)
    whole_population = rows_q.shape[0]
    left_q = jnp.transpose(
        rows_q.astype(jnp.float32) * every_weight[:, None, None], (1, 0, 2)
    ).reshape(rows_q.shape[1], whole_population * RANK)
    right_q = right_factors_gathered.astype(jnp.float32).reshape(
        whole_population * RANK, local_feats
    )
    grad_query = jnp.dot(left_q, right_q, precision=lax.Precision.HIGHEST) / noise_scale
    output_left_factor = jnp.transpose(
        left_all.astype(jnp.float32) * every_weight[:, None, None], (1, 0, 2)
    ).reshape(local_feats, whole_population * RANK)
    right_o = cols_o.astype(jnp.float32).reshape(whole_population * RANK, cols_o.shape[2])
    grad_out = jnp.dot(output_left_factor, right_o, precision=lax.Precision.HIGHEST) / noise_scale
    return (grad_query, grad_out, fitness)


def solution(mesh):
    placed = (
        P(),
        P(None, "mp"),
        P("pop", "mp"),
        P(None, "mp"),
        P(None, "mp"),
        P("mp", "pop"),
        P("pop", None, None),
        P("pop", None, "mp"),
        P("pop", "mp", None),
        P("pop", None, None),
        P("pop"),
    )
    return jax.shard_map(
        per_device,
        mesh=mesh,
        in_specs=placed,
        out_specs=(P("pop", "mp"), P("mp", "pop"), P("pop")),
        check_vma=False,
    )
```

profile of v0, /device:TPU:0, one launch (start us, length us, event | category | flops | bytes accessed | tf_op | source)
XLA Modules:
  0.0 465.0 jit_solution(14919115663158646740)
XLA Ops:
  12.2 101.0 %all-gather.3.cloned.1.call-done = bf16[3584,896]{1,0:T(8,128)(2,1)} async-done(((bf16[448,896]{1,0:T(8,128)(2,1)}), bf16[3584,896]{1,0:T(8,128)(2,1)}) %all-gather.3.cloned.1.call-update) | async-done | bytes 6422544 | tf_op jit(solution)/shard_map/all_gather | solution.py:57
  113.2 4.9 %fusion.37 = f32[256,896]{1,0:T(8,128)S(1)} fusion(bf16[256,3584]{1,0:T(8,128)(2,1)S(1)} %copy-done, bf16[3584,896]{1,0:T(8,128)(2,1)} %all-gather.3.cloned.1.call-done), kind=kOutput, calls=%fused_computation.66 | convolution fusion | flops 1644167168 | bytes 9175040 | tf_op jit(solution)/shard_map/dot_general | solution.py:55
  118.1 2.7 fusion.4
  129.5 2.9 convolution_convert_fusion
  132.5 81.4 %all-gather.5.cloned.1.call-done = bf16[896,3584]{0,1:T(8,128)(2,1)} async-done(((bf16[896,448]{0,1:T(8,128)(2,1)}), bf16[896,3584]{0,1:T(8,128)(2,1)}) %all-gather.5.cloned.1.call-update) | async-done | bytes 6422544 | tf_op jit(solution)/shard_map/all_gather | solution.py:96
  213.9 4.9 %fusion.38 = f32[256,3584]{1,0:T(8,128)S(1)} fusion(bf16[256,896]{0,1:T(8,128)(2,1)S(1)} %bitcast.110, bf16[896,3584]{0,1:T(8,128)(2,1)} %all-gather.5.cloned.1.call-done), kind=kOutput, calls=%fused_computation.67 | convolution fusion | flops 1644167168 | bytes 10551296 | tf_op jit(solution)/shard_map/mtf,fe->mte/dot_general | solution.py:93
  218.9 3.7 fusion.2
  222.6 8.8 %copy.54 = bf16[1,256,3584]{1,0,2:T(2,128)(2,1)} copy(bf16[1,256,3584]{2,1,0:T(8,128)(2,1)} %fusion.2) | data formatting | bytes 3670016
  231.4 3.6 copy.62
  235.0 3.2 copy.46
  238.8 20.8 %reduce.4 = bf16[3584,4]{1,0:T(8,128)(2,1)S(1)} reduce(bf16[3584,1,4]{2,1,0:T(2,128)(2,1)} %bitcast.105, bf16[]{:T(256)} %broadcast.87), dimensions={1}, to_apply=%bitcast.83.reduce_sub_computation | reduce | bytes 57346
  259.6 2.2 reshape.258
  261.8 3.6 all-to-all-start.1
  265.4 3.2 copy.37
  268.6 20.7 %reduce.3 = bf16[3584,4]{1,0:T(8,128)(2,1)S(1)} reduce(bf16[3584,1,4]{2,1,0:T(2,128)(2,1)} %bitcast.106, bf16[]{:T(256)} %broadcast.87), dimensions={1}, to_apply=%bitcast.81.reduce_sub_computation | reduce | bytes 57346
  289.3 2.2 reshape.256
  292.2 5.7 %all-to-all-start = ((bf16[8,2,896]{2,1,0:T(2,128)(2,1)}), bf16[8,2,896]{2,1,0:T(2,128)(2,1)S(1)}, u32[]{:S(2)}, u32[]{:S(2)}) async-start(bf16[8,2,896]{2,1,0:T(2,128)(2,1)} %reshape.256), calls=%async_computation | async-start | bytes 57344 | tf_op jit(solution)/shard_map/all_to_all | solution.py:117
  297.8 31.3 %all_gather.19 = bf16[8,896,4]{1,2,0:T(4,128)(2,1)S(1)} all-gather(bf16[1,896,4]{1,2,0:T(4,128)(2,1)S(1)} %copy-done.8), channel_id=1, replica_groups=mesh['pop'=8,'mp'=4] {'pop'}, dimensions={0}, use_global_device_ids=true | all-gather | bytes 64512 | tf_op jit(solution)/shard_map/all_gather | solution.py:115
  329.1 30.7 %all_gather.18 = bf16[8,4,896]{2,1,0:T(4,128)(2,1)S(1)} all-gather(bf16[1,4,896]{2,1,0:T(4,128)(2,1)S(1)} %copy-done.9), channel_id=1, replica_groups=mesh['pop'=8,'mp'=4] {'pop'}, dimensions={0}, use_global_device_ids=true | all-gather | bytes 64512 | tf_op jit(solution)/shard_map/all_gather | solution.py:114
  359.8 3.3 reshape.259
  363.2 3.6 copy.47
  367.0 3.3 reshape.257
  370.3 4.6 bitcast_convert_fusion
  378.0 1.9 fusion.8
  379.8 6.3 %psum.21 = f32[1]{0:T(128)} all-reduce(f32[1]{0:T(128)} %bitcast.27), channel_id=1, replica_groups=mesh['pop'=8,'mp'=4] {'mp'}, use_global_device_ids=true, to_apply=%region_4.5 | all-reduce | flops 1 | bytes 8 | tf_op jit(solution)/shard_map/psum | solution.py:106
  387.2 21.8 %psum.22 = f32[]{:T(128)} all-reduce(f32[]{:T(128)} %bitcast.28), channel_id=1, replica_groups=mesh['pop'=8,'mp'=4] {'pop'}, use_global_device_ids=true, to_apply=%region_5.6 | all-reduce | flops 1 | bytes 8 | tf_op jit(solution)/shard_map/psum | solution.py:109
  412.1 18.3 %psum.23 = f32[]{:T(128)} all-reduce(f32[]{:T(128)} %bitcast.30), channel_id=1, replica_groups=mesh['pop'=8,'mp'=4] {'pop'}, use_global_device_ids=true, to_apply=%region_6.7 | all-reduce | flops 1 | bytes 8 | tf_op jit(solution)/shard_map/psum | solution.py:110
  431.1 1.9 divide_dynamic-update-slice_fusion
  433.0 2.1 copy.44
  435.2 19.1 %all-reduce = f32[8]{0:T(128)S(1)} all-reduce(f32[8]{0:T(128)S(1)} %divide_dynamic-update-slice_fusion), channel_id=1, replica_groups=mesh['pop'=8,'mp'=4] {'pop'}, use_global_device_ids=true, to_apply=%add | all-reduce | flops 8 | bytes 64
  454.4 2.0 convolution_multiply_fusion.1
  456.4 2.1 bitcast_multiply_fusion
  (55 shorter events, 17.5 us)
Async XLA Ops:
  7.2 2.8 copy-start
  7.2 2.8 copy-start.2
  7.2 106.0 %all-gather.3.cloned.1.call-start = ((), (), s32[]{:S(2)}) async-start(), calls=%async_computation.3 | async-start | bytes 7225344 | tf_op jit(solution)/shard_map/all_gather | solution.py:57
  7.9 206.0 %all-gather.5.cloned.1.call-start = ((), (), s32[]{:S(2)}) async-start(), calls=%async_computation.4 | async-start | bytes 7225344 | tf_op jit(solution)/shard_map/all_gather | solution.py:96
  8.7 366.2 %reduce-scatter.4.cloned.1.call-start = ((), (), s32[]{:S(2)}) async-start(), calls=%async_computation.5 | async-start | bytes 2293760
  12.2 105.9 %copy-start.6 = (bf16[1,3584,4]{1,2,0:T(4,128)(2,1)S(1)}, bf16[1,3584,4]{1,2,0:T(4,128)(2,1)}, u32[]{:S(2)}) copy-start(bf16[1,3584,4]{1,2,0:T(4,128)(2,1)} %param.17) | copy-start | bytes 86020
  12.2 105.9 %copy-start.9 = (bf16[1,4,896]{2,1,0:T(4,128)(2,1)S(1)}, bf16[1,4,896]{2,1,0:T(4,128)(2,1)}, u32[]{:S(2)}) copy-start(bf16[1,4,896]{2,1,0:T(4,128)(2,1)} %param.18) | copy-start | bytes 21508
  125.9 1.4 copy-start.3
  125.9 1.4 copy-start.4
  127.9 1.2 copy-start.1
  129.4 2.9 copy-start.8
  132.5 86.4 %copy-start.5 = (bf16[1,4,3584]{2,1,0:T(4,128)(2,1)S(1)}, bf16[1,4,3584]{2,1,0:T(4,128)(2,1)}, u32[]{:S(2)}) copy-start(bf16[1,4,3584]{2,1,0:T(4,128)(2,1)} %param.20) | copy-start | bytes 86020
  238.8 26.6 %copy-start.7 = (bf16[1,3584,4]{1,2,0:T(4,128)(2,1)S(1)}, bf16[1,3584,4]{1,2,0:T(4,128)(2,1)}, u32[]{:S(2)}) copy-start(bf16[1,3584,4]{1,2,0:T(4,128)(2,1)} %param.17) | copy-start | bytes 86020
  261.8 30.4 %all-to-all-start.1 = ((bf16[8,2,896]{2,1,0:T(2,128)(2,1)}), bf16[8,2,896]{2,1,0:T(2,128)(2,1)S(1)}, u32[]{:S(2)}, u32[]{:S(2)}) async-start(bf16[8,2,896]{2,1,0:T(2,128)(2,1)} %reshape.258), calls=%async_computation.1 | async-start | bytes 57344 | tf_op jit(solution)/shard_map/all_to_all | solution.py:118
  268.6 23.0 %copy-start.10 = (u32[32]{0:T(128)S(1)}, u32[32]{0:T(128)}, u32[]{:S(2)}) copy-start(u32[32]{0:T(128)} %constant.59) | copy-start | bytes 388
  292.2 74.8 %all-to-all-start = ((bf16[8,2,896]{2,1,0:T(2,128)(2,1)}), bf16[8,2,896]{2,1,0:T(2,128)(2,1)S(1)}, u32[]{:S(2)}, u32[]{:S(2)}) async-start(bf16[8,2,896]{2,1,0:T(2,128)(2,1)} %reshape.256), calls=%async_computation | async-start | bytes 57344 | tf_op jit(solution)/shard_map/all_to_all | solution.py:117
Sparse Core Ops, SparseCore 0:
  10.2 103.0 all-gather.2
  115.4 98.4 all-gather.4
  235.2 27.7 reduce-scatter.3
where the time goes:
time: 466 us; the launch traced here: 465 us
  waiting for transfers between devices  184 us (39%)
  blocking collectives  127 us (27%)
  other arithmetic  53.7 us (12%)
  local copies, waits for them, and re-layouts  46.4 us (10%)
  matrix products  24.7 us (5%)
  between operations  19.6 us (4%)
  starting transfers between devices  9.34 us (2%)
    all_gather x1, waiting for transfers between devices, per_device(): lax.all_gather(w_query, 'pop', axis=0, tiled=True)  101 us
    all_gather x1, waiting for transfers between devices, per_device(): lax.all_gather(w_out, 'pop', axis=1, tiled=True)  81.4 us
    unnamed x3, other arithmetic  43.4 us
    unnamed x37, local copies, waits for them, and re-layouts  38 us
    all_gather x1, blocking collectives, per_device(): lax.all_gather(o_left, 'pop', axis=0, tiled=True)  31.3 us
    all_gather x1, blocking collectives, per_device(): lax.all_gather(query_right_factors, 'pop', axis=0, tiled=True)  30.7 us
    psum x1, blocking collectives, per_device(): mean = lax.psum(jnp.sum(fitness), 'pop') / count  21.8 us
    unnamed x1, blocking collectives  19.1 us
  transfers between devices with their start and end apart: 5, of which 2 were waited for; matrix products, arithmetic and copies ran while one was open for 19% of the time, Pallas kernels for 0%

commit v1 on v0

--- a/solution.py
+++ b/solution.py
@@ -12,6 +12,12 @@
 noise_scale = 0.5
 rope_base = 1000000.0
 spread_floor = 0.001
+
+
+def stack_and_merge(x, axis, dim):
+    parts = lax.all_gather(x, axis, axis=0, tiled=False)
+    whole = jnp.concatenate(parts, axis=dim)
+    return whole
 
 
 def tables(count, head_size):
@@ -91,10 +97,7 @@
     low_out = jnp.einsum("mtf,mfr->mtr", mixed, o_left, preferred_element_type=jnp.float32)
     right_full = o_right.astype(jnp.float32)
     part = jnp.einsum(
-        "mtf,fe->mte",
-        mixed,
-        lax.all_gather(w_out, "pop", axis=1, tiled=True),
-        preferred_element_type=jnp.float32,
+        "mtf,fe->mte", mixed, stack_and_merge(w_out, "pop", 1), preferred_element_type=jnp.float32
     )
     term = part + factor * jnp.einsum(
         "mtr,mre->mte", low_out, right_full, precision=lax.Precision.HIGHEST

time: 466 us -> 466 us (level)
  waiting for transfers between devices: 184 us -> 190 us
  other arithmetic: 53.7 us -> 48.9 us
    all_gather x1, waiting for transfers between devices: 81.4 us -> 87.5 us  [stack_and_merge(): parts = lax.all_gather(x, axis, axis=0, tiled=False)]
    unnamed x37 -> x46, local copies, waits for them, and re-layouts: 38 us -> 37.6 us
  transfers between devices with their start and end apart: 5 -> 5, of which waited for: 2 -> 2; matrix products, arithmetic and copies ran while one was open for 19% -> 16% of each run, Pallas kernels for 0% -> 0%
where the time goes in v1:
time: 466 us; the launch traced here: 465 us
  waiting for transfers between devices  190 us (41%)
  blocking collectives  127 us (27%)
  other arithmetic  48.9 us (10%)
  local copies, waits for them, and re-layouts  46.4 us (10%)
  matrix products  23.2 us (5%)
  between operations  19.7 us (4%)
  starting transfers between devices  9.46 us (2%)
    all_gather x1, waiting for transfers between devices, per_device(): lax.all_gather(w_query, 'pop', axis=0, tiled=True)  101 us
    all_gather x1, waiting for transfers between devices, stack_and_merge(): parts = lax.all_gather(x, axis, axis=0, tiled=False)  87.5 us
    unnamed x3, other arithmetic  41.4 us
    unnamed x46, local copies, waits for them, and re-layouts  37.6 us
    all_gather x1, blocking collectives, per_device(): lax.all_gather(o_left, 'pop', axis=0, tiled=True)  31.3 us
    all_gather x1, blocking collectives, per_device(): lax.all_gather(query_right_factors, 'pop', axis=0, tiled=True)  30.7 us
    psum x1, blocking collectives, per_device(): mean = lax.psum(jnp.sum(fitness), 'pop') / count  21.8 us
    unnamed x1, blocking collectives  19.1 us
  transfers between devices with their start and end apart: 5, of which 2 were waited for; matrix products, arithmetic and copies ran while one was open for 16% of the time, Pallas kernels for 0%

profile of v1, /device:TPU:0, one launch (start us, length us, event | category | flops | bytes accessed | tf_op | source)
XLA Modules:
  0.0 464.9 jit_solution(4772980862311053942)
XLA Ops:
  12.2 101.0 %all-gather.4.cloned.1.call-done = bf16[3584,896]{1,0:T(8,128)(2,1)} async-done(((bf16[448,896]{1,0:T(8,128)(2,1)}), bf16[3584,896]{1,0:T(8,128)(2,1)}) %all-gather.4.cloned.1.call-update) | async-done | bytes 6422544 | tf_op jit(solution)/shard_map/all_gather | solution.py:63
  113.2 4.9 %fusion.37 = f32[256,896]{1,0:T(8,128)S(1)} fusion(bf16[256,3584]{1,0:T(8,128)(2,1)S(1)} %copy-done, bf16[3584,896]{1,0:T(8,128)(2,1)} %all-gather.4.cloned.1.call-done), kind=kOutput, calls=%fused_computation.66 | convolution fusion | flops 1644167168 | bytes 9175040 | tf_op jit(solution)/shard_map/dot_general | solution.py:61
  118.1 2.7 fusion.4
  125.9 87.5 %all-gather.6.cloned.1.call-done = bf16[7168,448]{0,1:T(8,128)(2,1)} async-done(((bf16[896,448]{0,1:T(8,128)(2,1)}), bf16[7168,448]{0,1:T(8,128)(2,1)}) %all-gather.6.cloned.1.call-update) | async-done | bytes 6422544 | tf_op jit(solution)/shard_map/all_gather | solution.py:18
  213.3 4.3 copy.70
  217.6 3.8 copy.54
  224.6 2.6 convolution_convert_fusion
  227.2 4.9 %fusion.38 = f32[256,3584]{1,0:T(8,128)S(1)} fusion(bf16[256,896]{0,1:T(8,128)(2,1)S(1)} %bitcast.119, bf16[896,3584]{0,1:T(8,128)(2,1)} %bitcast.109), kind=kOutput, calls=%fused_computation.67 | convolution fusion | flops 1644167168 | bytes 10551296 | tf_op jit(solution)/shard_map/mtf,fe->mte/dot_general | solution.py:99
  232.3 2.5 fusion.2
  234.8 6.5 %copy.65 = bf16[1,256,3584]{1,0,2:T(2,128)(2,1)} copy(bf16[1,256,3584]{2,1,0:T(8,128)(2,1)S(1)} %fusion.2) | data formatting | bytes 3670016
  241.3 3.6 copy.74
  244.9 2.5 copy.57
  248.0 19.7 %reduce.4 = bf16[3584,4]{1,0:T(8,128)(2,1)S(1)} reduce(bf16[3584,1,4]{2,1,0:T(2,128)(2,1)S(1)} %bitcast.114, bf16[]{:T(256)} %broadcast.87), dimensions={1}, to_apply=%bitcast.90.reduce_sub_computation | reduce | bytes 57346
  267.7 2.2 reshape.267
  269.9 3.6 all-to-all-start.1
  273.5 2.5 copy.47
  276.1 19.7 %reduce.3 = bf16[3584,4]{1,0:T(8,128)(2,1)S(1)} reduce(bf16[3584,1,4]{2,1,0:T(2,128)(2,1)S(1)} %bitcast.115, bf16[]{:T(256)} %broadcast.87), dimensions={1}, to_apply=%bitcast.88.reduce_sub_computation | reduce | bytes 57346
  295.8 2.2 reshape.265
  298.6 5.8 %all-to-all-start = ((bf16[8,2,896]{2,1,0:T(2,128)(2,1)}), bf16[8,2,896]{2,1,0:T(2,128)(2,1)S(1)}, u32[]{:S(2)}, u32[]{:S(2)}) async-start(bf16[8,2,896]{2,1,0:T(2,128)(2,1)} %reshape.265), calls=%async_computation | async-start | bytes 57344 | tf_op jit(solution)/shard_map/all_to_all | solution.py:120
  304.4 31.3 %all_gather.23 = bf16[8,896,4]{1,2,0:T(4,128)(2,1)S(1)} all-gather(bf16[1,896,4]{1,2,0:T(4,128)(2,1)S(1)} %copy-done.11), channel_id=1, replica_groups=mesh['pop'=8,'mp'=4] {'pop'}, dimensions={0}, use_global_device_ids=true | all-gather | bytes 64512 | tf_op jit(solution)/shard_map/all_gather | solution.py:118
  335.6 30.7 %all_gather.22 = bf16[8,4,896]{2,1,0:T(4,128)(2,1)S(1)} all-gather(bf16[1,4,896]{2,1,0:T(4,128)(2,1)S(1)} %copy-done.12), channel_id=1, replica_groups=mesh['pop'=8,'mp'=4] {'pop'}, dimensions={0}, use_global_device_ids=true | all-gather | bytes 64512 | tf_op jit(solution)/shard_map/all_gather | solution.py:117
  366.4 2.3 reshape.268
  370.7 2.4 reshape.266
  373.1 3.0 bitcast_convert_fusion
  379.3 1.9 fusion.8
  381.2 6.3 %psum.21 = f32[1]{0:T(128)} all-reduce(f32[1]{0:T(128)} %bitcast.29), channel_id=1, replica_groups=mesh['pop'=8,'mp'=4] {'mp'}, use_global_device_ids=true, to_apply=%region_4.5 | all-reduce | flops 1 | bytes 8 | tf_op jit(solution)/shard_map/psum | solution.py:109
  388.6 21.8 %psum.22 = f32[]{:T(128)} all-reduce(f32[]{:T(128)} %bitcast.30), channel_id=1, replica_groups=mesh['pop'=8,'mp'=4] {'pop'}, use_global_device_ids=true, to_apply=%region_5.6 | all-reduce | flops 1 | bytes 8 | tf_op jit(solution)/shard_map/psum | solution.py:112
  413.5 18.3 %psum.23 = f32[]{:T(128)} all-reduce(f32[]{:T(128)} %bitcast.32), channel_id=1, replica_groups=mesh['pop'=8,'mp'=4] {'pop'}, use_global_device_ids=true, to_apply=%region_6.7 | all-reduce | flops 1 | bytes 8 | tf_op jit(solution)/shard_map/psum | solution.py:113
  432.5 2.0 divide_dynamic-update-slice_fusion
  435.1 19.1 %all-reduce = f32[8]{0:T(128)S(1)} all-reduce(f32[8]{0:T(128)S(1)} %divide_dynamic-update-slice_fusion), channel_id=1, replica_groups=mesh['pop'=8,'mp'=4] {'pop'}, use_global_device_ids=true, to_apply=%add | all-reduce | flops 8 | bytes 64
  454.4 2.0 convolution_multiply_fusion.1
  456.3 2.1 bitcast_multiply_fusion
  (65 shorter events, 19.8 us)
Async XLA Ops:
  7.2 2.8 copy-start
  7.2 2.8 copy-start.5
  7.2 106.0 %all-gather.4.cloned.1.call-start = ((), (), s32[]{:S(2)}) async-start(), calls=%async_computation.3 | async-start | bytes 7225344 | tf_op jit(solution)/shard_map/all_gather | solution.py:63
  7.9 205.4 %all-gather.6.cloned.1.call-start = ((), (), s32[]{:S(2)}) async-start(), calls=%async_computation.4 | async-start | bytes 7225344 | tf_op jit(solution)/shard_map/all_gather | solution.py:18
  8.7 367.4 %reduce-scatter.4.cloned.1.call-start = ((), (), s32[]{:S(2)}) async-start(), calls=%async_computation.5 | async-start | bytes 2293760
  12.2 105.9 %copy-start.9 = (bf16[1,3584,4]{1,2,0:T(4,128)(2,1)S(1)}, bf16[1,3584,4]{1,2,0:T(4,128)(2,1)}, u32[]{:S(2)}) copy-start(bf16[1,3584,4]{1,2,0:T(4,128)(2,1)} %param.17) | copy-start | bytes 86020
  12.2 105.9 %copy-start.12 = (bf16[1,4,896]{2,1,0:T(4,128)(2,1)S(1)}, bf16[1,4,896]{2,1,0:T(4,128)(2,1)}, u32[]{:S(2)}) copy-start(bf16[1,4,896]{2,1,0:T(4,128)(2,1)} %param.18) | copy-start | bytes 21508
  217.6 3.8 copy-start.4
  221.4 0.8 copy-start.6
  221.4 0.8 copy-start.7
  222.8 1.3 copy-start.3
  222.8 1.8 copy-start.13
  227.2 5.0 %copy-start.11 = (bf16[1,896,4]{1,2,0:T(4,128)(2,1)S(1)}, bf16[1,896,4]{1,2,0:T(4,128)(2,1)}, u32[]{:S(2)}) copy-start(bf16[1,896,4]{1,2,0:T(4,128)(2,1)} %param.19) | copy-start | bytes 21508
  227.2 5.1 %copy-start.8 = (bf16[1,4,3584]{2,1,0:T(4,128)(2,1)S(1)}, bf16[1,4,3584]{2,1,0:T(4,128)(2,1)}, u32[]{:S(2)}) copy-start(bf16[1,4,3584]{2,1,0:T(4,128)(2,1)} %param.20) | copy-start | bytes 86020
  248.0 25.5 %copy-start.10 = (bf16[1,3584,4]{1,2,0:T(4,128)(2,1)S(1)}, bf16[1,3584,4]{1,2,0:T(4,128)(2,1)}, u32[]{:S(2)}) copy-start(bf16[1,3584,4]{1,2,0:T(4,128)(2,1)} %param.17) | copy-start | bytes 86020
  269.9 28.7 %all-to-all-start.1 = ((bf16[8,2,896]{2,1,0:T(2,128)(2,1)}), bf16[8,2,896]{2,1,0:T(2,128)(2,1)S(1)}, u32[]{:S(2)}, u32[]{:S(2)}) async-start(bf16[8,2,896]{2,1,0:T(2,128)(2,1)} %reshape.267), calls=%async_computation.1 | async-start | bytes 57344 | tf_op jit(solution)/shard_map/all_to_all | solution.py:121
  276.0 21.9 %copy-start.14 = (u32[32]{0:T(128)S(1)}, u32[32]{0:T(128)}, u32[]{:S(2)}) copy-start(u32[32]{0:T(128)} %constant.59) | copy-start | bytes 388
  298.6 72.1 %all-to-all-start = ((bf16[8,2,896]{2,1,0:T(2,128)(2,1)}), bf16[8,2,896]{2,1,0:T(2,128)(2,1)S(1)}, u32[]{:S(2)}, u32[]{:S(2)}) async-start(bf16[8,2,896]{2,1,0:T(2,128)(2,1)} %reshape.265), calls=%async_computation | async-start | bytes 57344 | tf_op jit(solution)/shard_map/all_to_all | solution.py:120
  376.1 58.3 %copy-start.2 = (f32[1,3584,4]{2,0,1:T(1,128)S(1)}, f32[1,3584,4]{2,0,1:T(1,128)}, u32[]{:S(2)}) copy-start(f32[1,3584,4]{2,0,1:T(1,128)} %bitcast_convert_fusion) | copy-start | bytes 172036
  454.3 4.1 copy-start.1
Sparse Core Ops, SparseCore 0:
  10.2 103.0 all-gather.3
  115.4 97.9 all-gather.5
  245.1 28.3 reduce-scatter.3
